TPU v7x, 32 devices: a whole 2x2x4 slice. The times are simulated.
32 devices in a mesh: dev: 8 (over z, x), rep: 4 (over y, core).
Axes of the slice: x: 2, y: 2, z: 4, core: 2. Of those that a mesh axis runs over, the one named last changes fastest.
Arguments:
- h_zero: bfloat16 [32768, 256], P(('dev', 'rep')), may hold values from 0 to 2
- h_prev: bfloat16 [32768, 256], P(('dev', 'rep')), may hold values from 0 to 2
- hist_a: bfloat16 [32768, 256], P('dev'), may hold values from 0 to 2
- hist_b: bfloat16 [32768, 256], P('dev'), may hold values from 0 to 2
- tile_vals: bfloat16 [256, 12, 128, 128], P(('dev', 'rep'))
- tile_cols: int32 [256, 12], P(('dev', 'rep')), may hold values from 0 to 47, as said below
- pull_rows: int32 [32, 8, 128], P(('dev', 'rep')), may hold values from 0 to 4095
- pull_counts: int32 [32, 8], P(('dev', 'rep')), may hold values from 96 to 128, as said below
- weight_two: bfloat16 [256, 256], replicated, may hold values from -0.375 to 0.375
- weight_three: bfloat16 [256, 256], replicated, may hold values from -0.375 to 0.375
- grad_out: bfloat16 [32768, 256], P(('dev', 'rep')), may hold values from -0.125 to 0.125
Outputs:
- layer_three: bfloat16 [32768, 256], P(('dev', 'rep'))
- new_history: bfloat16 [32768, 256], P('dev')
- weight_grad: float32 [256, 256], replicated
Inputs may be any that keep to these rules, and one draw needn't show every extreme that they name: `tile_cols`: entry 0 of a row block names one of its device's own 8 blocks; entries 1 to 3 name blocks of the owner's history shard; the other 8 name pulled blocks of consecutive owners modulo 8, and every owner's block is named by some row block of each device. `pull_rows`: entries at slots at or past the block's count are read by no output. `pull_counts`: every device pulls a full block of 128 rows from some owner and a block of exactly 96 rows from another.
All inputs are finite; a program needn't handle non-finite values.
Results may differ from a plain program's by a relative error of at most 0.0034.
Values may be sent and summed in bfloat16 or wider, within the bound.
A program may use at most 128 MiB of HBM per device.

v0:
```python
import math

import jax
import jax.numpy as jnp
from jax import lax
from jax.sharding import PartitionSpec as P

restart = 0.1
strength = 0.5


def propagate(current, history, pulled, values, columns, start_rows, weight, layer_number):
    feature_width = current.shape[1]
    tile_size = values.shape[2]
    source = jnp.concatenate([current, history, pulled.reshape(-1, feature_width)], axis=0)
    blocks = source.reshape(-1, tile_size, feature_width)
    picked = jnp.take(blocks, columns.reshape(-1), axis=0).reshape(
        columns.shape + (tile_size, feature_width)
    )
    summed = jnp.einsum("btij,btjf->bif", values, picked, preferred_element_type=jnp.float32)
    summed = summed.reshape(current.shape[0], feature_width)
    mixed_rows = (1.0 - restart) * summed + restart * start_rows.astype(jnp.float32)
    mixed_low = mixed_rows.astype(jnp.bfloat16)
    factor = math.log(strength / layer_number + 1.0)
    product = jnp.dot(mixed_low, weight, preferred_element_type=jnp.float32)
    inner_sum = (1.0 - factor) * mixed_rows + factor * product
    return (jnp.maximum(inner_sum, 0.0).astype(jnp.bfloat16), mixed_low)


def local(
    h_zero,
    h_prev,
    hist_a,
    hist_b,
    tile_vals,
    tile_cols,
    pull_rows,
    pull_counts,
    weight_two,
    weight_three,
    grad_out,
):
    wanted = pull_rows[0]
    peer_count, slot_count = wanted.shape
    feature_width = hist_a.shape[1]
    asked_rows = lax.all_to_all(wanted, "dev", split_axis=0, concat_axis=0, tiled=True)
    flat_rows = asked_rows.reshape(-1)
    live_mask = (lax.broadcasted_iota(jnp.int32, wanted.shape, 1) < pull_counts[0][:, None])[
        :, :, None
    ]

    def serve_rows(history):
        return jnp.take(history, flat_rows, axis=0).reshape(peer_count, slot_count, feature_width)

    def trim_rows(arrived):
        return jnp.where(live_mask, arrived, jnp.zeros((), jnp.bfloat16))

    reply_a = lax.all_to_all(serve_rows(hist_a), "dev", split_axis=0, concat_axis=0, tiled=True)
    second, unused_mix = propagate(
        h_prev, hist_a, trim_rows(reply_a), tile_vals, tile_cols, h_zero, weight_two, 2
    )
    reply_b = lax.all_to_all(serve_rows(hist_b), "dev", split_axis=0, concat_axis=0, tiled=True)
    fresh_rows = lax.all_gather(second, "rep", axis=0, tiled=True)
    layer_three, mixed_low = propagate(
        second, hist_b, trim_rows(reply_b), tile_vals, tile_cols, h_zero, weight_three, 3
    )
    factor = math.log(strength / 3 + 1.0)
    grad_term = factor * lax.dot_general(
        mixed_low, grad_out, (((0,), (0,)), ((), ())), preferred_element_type=jnp.float32
    )
    grad_total = lax.psum(grad_term, ("dev", "rep"))
    return (layer_three, fresh_rows, grad_total)


def solution(mesh):
    return jax.shard_map(
        local,
        mesh=mesh,
        in_specs=(
            P(("dev", "rep"), None),
            P(("dev", "rep"), None),
            P("dev", None),
            P("dev", None),
            P(("dev", "rep"), None, None, None),
            P(("dev", "rep"), None),
            P(("dev", "rep"), None, None),
            P(("dev", "rep"), None),
            P(),
            P(),
            P(("dev", "rep"), None),
        ),
        out_specs=(P(("dev", "rep"), None), P("dev", None), P()),
        check_vma=False,
    )
```

profile of v0, /device:TPU:0, one launch (start us, length us, event | category | flops | bytes accessed | tf_op | source)
XLA Modules:
  0.0 246.1 jit_solution(17458504703795671243)
XLA Ops:
  8.0 14.0 %all_to_all.19 = s32[8,1,128]{2,1,0:T(1,128)S(1)} all-to-all(s32[8,1,128]{2,1,0:T(1,128)} %bitcast.46), channel_id=1, replica_groups=mesh['dev'=8,'rep'=4] {'dev'}, dimensions={0} | all-to-all | bytes 8192 | tf_op jit(solution)/shard_map/all_to_all | solution.py:46
  22.0 6.5 %gather_fusion = bf16[1024,256]{1,0:T(8,128)(2,1)} fusion(bf16[4096,256]{1,0:T(8,128)(2,1)} %param.17, s32[1024]{0:T(1024)S(1)} %fusion.11), kind=kCustom, calls=%fused_computation.clone | custom fusion | bytes 1052672 | tf_op jit(solution)/shard_map/jit(_take)/gather | solution.py:53
  28.5 6.5 %gather_fusion.2 = bf16[1024,256]{1,0:T(8,128)(2,1)} fusion(bf16[4096,256]{1,0:T(8,128)(2,1)} %param.18, s32[1024]{0:T(1024)S(1)} %fusion.11), kind=kCustom, calls=%fused_computation.2.clone | custom fusion | bytes 1052672 | tf_op jit(solution)/shard_map/jit(_take)/gather | solution.py:53
  35.0 2.2 broadcast_select_fusion.3
  37.2 16.4 %all_to_all.20 = bf16[8,128,256]{2,1,0:T(8,128)(2,1)} all-to-all(bf16[8,128,256]{2,1,0:T(8,128)(2,1)S(1)} %bitcast.43), channel_id=1, replica_groups=mesh['dev'=8,'rep'=4] {'dev'}, dimensions={0} | all-to-all | bytes 1048576 | tf_op jit(solution)/shard_map/all_to_all | solution.py:58
  53.6 4.1 %all-to-all-start.2 = ((bf16[8,128,256]{2,1,0:T(8,128)(2,1)}), bf16[8,128,256]{2,1,0:T(8,128)(2,1)}, u32[]{:S(2)}, u32[]{:S(2)}) async-start(bf16[8,128,256]{2,1,0:T(8,128)(2,1)} %bitcast.42), calls=%async_computation.2 | async-start | bytes 1048576 | tf_op jit(solution)/shard_map/all_to_all | solution.py:62
  58.0 13.4 %all-to-all-done.2 = bf16[8,128,256]{2,1,0:T(8,128)(2,1)} async-done(((bf16[8,128,256]{2,1,0:T(8,128)(2,1)}), bf16[8,128,256]{2,1,0:T(8,128)(2,1)}, u32[]{:S(2)}, u32[]{:S(2)}) %all-to-all-start.2) | async-done | bytes 524320 | tf_op jit(solution)/shard_map/all_to_all | solution.py:62
  71.4 2.2 broadcast_select_fusion.5
  73.6 3.1 %pad_maximum_fusion = bf16[6144,256]{1,0:T(8,128)(2,1)} fusion(bf16[1024,256]{1,0:T(8,128)(2,1)S(1)} %bitcast.41, bf16[4096,256]{1,0:T(8,128)(2,1)} %param.17, bf16[1024,256]{1,0:T(8,128)(2,1)} %param.16), kind=kLoop, calls=%fused_computation.6 | loop fusion | flops 9437184 | bytes 6291456 | tf_op jit(solution)/shard_map/concatenate | solution.py:15
  76.7 7.9 %gather_fusion.1 = bf16[96,128,256]{2,1,0:T(8,128)(2,1)} fusion(bf16[48,128,256]{2,1,0:T(8,128)(2,1)} %bitcast.39, s32[1024]{0:T(1024)S(1)} %pad_clamp_fusion), kind=kCustom, calls=%fused_computation.1.clone | custom fusion | bytes 12583296 | tf_op jit(solution)/shard_map/jit(_take)/gather | solution.py:17
  84.6 3.4 %broadcast_select_fusion = bf16[96,128,256]{2,1,0:T(8,128)(2,1)S(1)} fusion(bf16[96,128,256]{2,1,0:T(8,128)(2,1)} %gather_fusion.1, pred[96]{0:T(512)(128)(4,1)S(1)} %compare_and_fusion.1), kind=kLoop, calls=%fused_computation.4 | loop fusion | flops 3145728 | bytes 12583008 | tf_op jit(solution)/shard_map/jit(_take)/select_n | solution.py:17
  88.1 1.2 fusion.1
  89.5 1.2 fusion.6
  90.7 3.2 %pad_maximum_fusion.1 = bf16[6144,256]{1,0:T(8,128)(2,1)} fusion(bf16[1024,256]{1,0:T(8,128)(2,1)} %bitcast.40, bf16[4096,256]{1,0:T(8,128)(2,1)} %param.18, bf16[1024,256]{1,0:T(8,128)(2,1)} %fusion.6), kind=kLoop, calls=%fused_computation.7 | loop fusion | flops 9437184 | bytes 6291456 | tf_op jit(solution)/shard_map/concatenate | solution.py:15
  93.9 7.9 %gather_fusion.3 = bf16[96,128,256]{2,1,0:T(8,128)(2,1)} fusion(bf16[48,128,256]{2,1,0:T(8,128)(2,1)} %bitcast.38, s32[1024]{0:T(1024)S(1)} %pad_clamp_fusion), kind=kCustom, calls=%fused_computation.3.clone | custom fusion | bytes 12583296 | tf_op jit(solution)/shard_map/jit(_take)/gather | solution.py:17
  101.8 3.4 %broadcast_select_fusion.1 = bf16[96,128,256]{2,1,0:T(8,128)(2,1)S(1)} fusion(bf16[96,128,256]{2,1,0:T(8,128)(2,1)} %gather_fusion.3, pred[96]{0:T(512)(128)(4,1)S(1)} %compare_and_fusion.1), kind=kLoop, calls=%fused_computation.5 | loop fusion | flops 3145728 | bytes 12583008 | tf_op jit(solution)/shard_map/jit(_take)/select_n | solution.py:17
  105.3 1.2 fusion
  106.7 1.0 copy-done.1
  107.7 1.0 convolution_multiply_fusion.2
  108.8 2.7 %fusion.7 = bf16[1024,256]{1,0:T(8,128)(2,1)} fusion(bf16[256,256]{1,0:T(8,128)(2,1)S(1)} %copy-done.6, f32[1024,256]{1,0:T(8,128)} %copy-done.1), kind=kOutput, calls=%fused_computation.19 | convolution fusion | flops 135790592 | bytes 1703936 | tf_op jit(solution)/shard_map/dot_general | solution.py:25
  111.4 1.0 all-gather.2.cloned.1.call-done
  112.5 121.5 %all-reduce.2.cloned.1.call-done = f32[256,256]{1,0:T(8,128)} async-done(((f32[256,256]{1,0:T(8,128)}), f32[256,256]{1,0:T(8,128)}) %all-reduce.2.cloned.1.call-update) | async-done | bytes 262160 | tf_op jit(solution)/shard_map/psum | solution.py:71
  233.9 3.0 %copy.18 = bf16[4096,256]{1,0:T(8,128)(2,1)} copy(bf16[4096,256]{1,0:T(8,128)(2,1)} %all-gather.2.cloned.1.call-done) | data formatting | bytes 4194304
  237.0 1.7 copy.19
  (30 shorter events, 0.6 us)
Async XLA Ops:
  8.0 80.1 %copy-start = (bf16[8,12,128,128]{3,2,1,0:T(8,128)(2,1)S(1)}, bf16[8,12,128,128]{3,2,1,0:T(8,128)(2,1)}, u32[]{:S(2)}) copy-start(bf16[8,12,128,128]{3,2,1,0:T(8,128)(2,1)} %param.19) | copy-start | bytes 9437188
  22.0 35.8 %copy-start.7 = (s32[8,12]{1,0:T(8,128)S(1)}, s32[8,12]{1,0:T(8,128)}, u32[]{:S(2)}) copy-start(s32[8,12]{1,0:T(8,128)} %param.20) | copy-start | bytes 1156
  22.0 35.9 %copy-start.8 = (s32[1,8]{1,0:T(1,128)S(1)}, s32[1,8]{1,0:T(1,128)}, u32[]{:S(2)}) copy-start(s32[1,8]{1,0:T(1,128)} %param.22) | copy-start | bytes 100
  53.6 17.8 %all-to-all-start.2 = ((bf16[8,128,256]{2,1,0:T(8,128)(2,1)}), bf16[8,128,256]{2,1,0:T(8,128)(2,1)}, u32[]{:S(2)}, u32[]{:S(2)}) async-start(bf16[8,128,256]{2,1,0:T(8,128)(2,1)} %bitcast.42), calls=%async_computation.2 | async-start | bytes 1048576 | tf_op jit(solution)/shard_map/all_to_all | solution.py:62
  57.7 54.7 %all-gather.2.cloned.1.call-start = ((), (), s32[]{:S(2)}) async-start(), calls=%async_computation.3 | async-start | bytes 2621440 | tf_op jit(solution)/shard_map/all_gather | solution.py:63
  88.1 1.3 copy-start.2
  88.1 1.4 copy-start.5
  90.6 143.3 %all-reduce.2.cloned.1.call-start = ((), (), s32[]{:S(2)}) async-start(), calls=%async_computation.4 | async-start | bytes 524288 | tf_op jit(solution)/shard_map/psum | solution.py:71
  105.3 1.3 copy-start.3
  105.3 2.4 copy-start.4
  105.3 3.4 %copy-start.6 = (bf16[256,256]{1,0:T(8,128)(2,1)S(1)}, bf16[256,256]{1,0:T(8,128)(2,1)}, u32[]{:S(2)}) copy-start(bf16[256,256]{1,0:T(8,128)(2,1)} %param.24) | copy-start | bytes 393220
  106.7 1.0 copy-start.1
Sparse Core Ops, SparseCore 0:
  90.8 21.6 all-gather.1
Sparse Core Ops, SparseCore 1:
  108.8 125.0 all-reduce.1
where the time goes:
time: 247 us; the launch traced here: 246 us
  waiting for transfers between devices  136 us (55%)
  local copies, waits for them, and re-layouts  34.6 us (14%)
  blocking collectives  30.4 us (12%)
  other arithmetic  17.9 us (7%)
  between operations  15.7 us (6%)
  matrix products  7.34 us (3%)
  starting transfers between devices  4.23 us (2%)
    psum x1, waiting for transfers between devices, local(): grad_total = lax.psum(grad_term, ('dev', 'rep'))  121 us
    all_to_all x1, blocking collectives, local(): lax.all_to_all(serve_rows(hist_a), 'dev', split_axis=0, concat_axis=0, ti...  16.4 us
    gather x2, local copies, waits for them, and re-layouts, propagate(): jnp.take(blocks, columns.reshape(-1), axis=0)  15.8 us
    all_to_all x1, blocking collectives, local(): lax.all_to_all(wanted, 'dev', split_axis=0, concat_axis=0, tiled=True)  14 us
    all_to_all x1, waiting for transfers between devices, local(): lax.all_to_all(serve_rows(hist_b), 'dev', split_axis=0, concat_axis=0, ti...  13.4 us
    gather x2, local copies, waits for them, and re-layouts, serve_rows(): jnp.take(history, flat_rows, axis=0)  13 us
    select_n x3, other arithmetic, propagate(): jnp.take(blocks, columns.reshape(-1), axis=0)  6.86 us
    concatenate x2, other arithmetic, propagate(): jnp.concatenate([current, history, pulled.reshape(-1, feature_width)], ax...  6.33 us
  transfers between devices with their start and end apart: 3, of which 3 were waited for; matrix products, arithmetic and copies ran while one was open for 8% of the time, Pallas kernels for 0%

commit v1 on v0

v1 whole, which is shorter than its diff:
```python
import functools
import math

import jax
import jax.numpy as jnp
from jax import lax
from jax.experimental import pallas as pl
from jax.experimental.pallas import tpu as pltpu
from jax.sharding import PartitionSpec as P

restart = 0.1
strength = 0.5
MESH = pl.DeviceIdType.MESH


def kernel(
    D, R,
    cols, counts, rows_in,
    h_zero, h_prev, hist_a, hist_b, tile_vals, w_two, w_three, grad_out,
    layer_out, hist_out, grad_res,
    zero_v, cur_v, hist_av, hist_bv, vals_v, w2_v, w3_v, up_v,
    ask, asked, col, send_a, send_b, pull_a, pull_b, acc, acc_a, acc_b,
    fresh, low_v, out_v, g_send, g_recv, g_part, g_all,
    local_sem, idx_s, idx_r, a_s, a_r, b_s, b_r, f_s, f_r, out_sem, g_s, g_r, p_s, p_r,
):
    N = D * R
    d = lax.axis_index("dev")
    r = lax.axis_index("rep")
    me = d * R + r
    slots = rows_in.shape[2]
    feat = hist_av.shape[2]
    blocks = vals_v.shape[0]
    tiles = vals_v.shape[1]
    home = 4
    home_blocks = hist_av.shape[0]

    loads = [
        (hist_a, hist_av), (tile_vals, vals_v), (h_prev, cur_v), (hist_b, hist_bv),
        (h_zero, zero_v), (w_two, w2_v), (w_three, w3_v), (grad_out, up_v),
    ]
    copies = [pltpu.make_async_copy(s, t, local_sem.at[i]) for i, (s, t) in enumerate(loads)]
    for c in copies:
        c.start()

    barrier = pltpu.get_barrier_semaphore()

    def greet(k, _):
        t = lax.rem(me + 1 + k, N)
        pl.semaphore_signal(
            barrier, inc=1, device_id=(lax.div(t, R), lax.rem(t, R)), device_id_type=MESH
        )
        return 0

    lax.fori_loop(0, N - 1, greet, 0)

    lane = lax.broadcasted_iota(jnp.int32, (1, slots), 1)

    def mask_rows(p, _):
        ask[p] = jnp.where(lane < counts[0, p], rows_in[0, pl.ds(p, 1), :], -1)
        return 0

    lax.fori_loop(0, D, mask_rows, 0)
    pl.semaphore_wait(barrier, N - 1)

    def send_rows(j, _):
        p = lax.rem(d + 1 + j, D)
        pltpu.make_async_remote_copy(
            src_ref=ask.at[p], dst_ref=asked.at[d], send_sem=idx_s, recv_sem=idx_r,
            device_id=(p, r), device_id_type=MESH,
        ).start()
        return 0

    lax.fori_loop(0, D - 1, send_rows, 0)
    asked[d] = ask[d]

    def whole(ref, n, s, q):
        part = ref.at[pl.ds(0, n)]
        return pltpu.make_async_remote_copy(
            src_ref=part, dst_ref=part, send_sem=s, recv_sem=q,
            device_id=(lax.rem(d + 1, D), r), device_id_type=MESH,
        )

    whole(asked, D - 1, idx_s, idx_r).wait_recv()

    def column(j, _):
        q = lax.rem(d + D - 1 - j + D, D)
        col[j] = jnp.broadcast_to(asked[q], (slots, slots)).T
        return 0

    lax.fori_loop(0, D, column, 0)

    group = 4 if D % 4 == 0 else 1
    chunk_blocks = 8
    depth = chunk_blocks * slots
    lanes = lax.broadcasted_iota(jnp.int32, (group * slots, depth), 1)

    def gather(table, send_buf, pull_buf, s, q_sem):
        def one_group(g, _):
            keys = col[pl.ds(g * group, group)].reshape(group * slots, slots)
            wide = jnp.concatenate([keys] * chunk_blocks, axis=1)

            def one_chunk(k, _):
                hot = jnp.where(wide - k * depth == lanes, 1.0, 0.0).astype(jnp.bfloat16)
                part = table[pl.ds(k * chunk_blocks, chunk_blocks)].reshape(depth, feat)
                found = jnp.dot(hot, part, preferred_element_type=jnp.float32)

                @pl.when(k == 0)
                def _():
                    acc[...] = found

                @pl.when(k > 0)
                def _():
                    acc[...] += found

                return 0

            lax.fori_loop(0, home_blocks // chunk_blocks, one_chunk, 0)
            send_buf[pl.ds(g * group, group)] = (
                acc[...].astype(jnp.bfloat16).reshape(group, slots, feat)
            )

            def send_one(i, _):
                j = g * group + i

                @pl.when(j < D - 1)
                def _():
                    q = lax.rem(d + D - 1 - j + D, D)
                    pltpu.make_async_remote_copy(
                        src_ref=send_buf.at[j], dst_ref=pull_buf.at[d], send_sem=s, recv_sem=q_sem,
                        device_id=(q, r), device_id_type=MESH,
                    ).start()

                return 0

            lax.fori_loop(0, group, send_one, 0)
            return 0

        lax.fori_loop(0, D // group, one_group, 0)
        pull_buf[d] = send_buf[D - 1]

    copies[0].wait()
    gather(hist_av, send_a, pull_a, a_s, a_r)
    copies[3].wait()
    gather(hist_bv, send_b, pull_b, b_s, b_r)
    for i in (1, 2, 4, 5, 6, 7):
        copies[i].wait()

    def product(i, picks):
        left = jnp.concatenate([vals_v[i, t] for t, _ in picks], axis=1)
        right = jnp.concatenate([b for _, b in picks], axis=0)
        return jnp.dot(left, right, preferred_element_type=jnp.float32)

    far_base = blocks + home_blocks

    def near(i, _):
        picks = [(0, cur_v[cols[i, 0]])]
        picks += [(t, hist_av[jnp.maximum(cols[i, t] - blocks, 0)]) for t in range(1, home)]
        acc_a[i] = product(i, picks)
        acc_b[i] = product(i, [(t, hist_bv[jnp.maximum(cols[i, t] - blocks, 0)]) for t in range(1, home)])
        return 0

    lax.fori_loop(0, blocks, near, 0)

    def finish(i, acc_ref, pull_buf, w, number, factor_weight):
        far = product(i, [(t, pull_buf[jnp.maximum(cols[i, t] - far_base, 0)]) for t in range(home, tiles)])
        summed = acc_ref[i] + far
        mixed = (1.0 - restart) * summed + restart * zero_v[i].astype(jnp.float32)
        low = mixed.astype(jnp.bfloat16)
        prod = jnp.dot(low, w[...], preferred_element_type=jnp.float32)
        inner = (1.0 - factor_weight) * mixed + factor_weight * prod
        return jnp.maximum(inner, 0.0).astype(jnp.bfloat16), low

    whole(pull_a, D - 1, a_s, a_r).wait_recv()
    factor_two = math.log(strength / 2 + 1.0)
    factor_three = math.log(strength / 3 + 1.0)

    def second(i, _):
        fresh[i] = finish(i, acc_a, pull_a, w2_v, 2, factor_two)[0]
        return 0

    lax.fori_loop(0, blocks, second, 0)

    def fresh_copy(src, slot, target, k):
        return pltpu.make_async_remote_copy(
            src_ref=src, dst_ref=hist_out.at[slot], send_sem=f_s.at[k], recv_sem=f_r.at[k],
            device_id=(d, target), device_id_type=MESH,
        )

    keep = pltpu.make_async_copy(fresh, hist_out.at[r], out_sem.at[0])
    if R == 4:
        mate = r + 1 - 2 * lax.rem(r, 2)
        across = lax.rem(r + 2, R)
        sends = [fresh_copy(fresh, r, across, 0), fresh_copy(fresh, r, mate, 1)]
        forward = fresh_copy(hist_out.at[across], across, mate, 2)
    else:
        sends = [fresh_copy(fresh, r, lax.rem(r + 1 + k, R), k) for k in range(R - 1)]
        forward = None
    for c in sends:
        c.start()
    keep.start()

    def own_tile(i, _):
        acc_b[i] += product(i, [(0, fresh[cols[i, 0]])])
        return 0

    lax.fori_loop(0, blocks, own_tile, 0)
    whole(pull_b, D - 1, b_s, b_r).wait_recv()

    def third(i, _):
        out, low = finish(i, acc_b, pull_b, w3_v, 3, factor_three)
        out_v[i] = out
        low_v[i] = low
        return 0

    lax.fori_loop(0, blocks, third, 0)
    put = pltpu.make_async_copy(out_v, layer_out, out_sem.at[1])
    put.start()

    grad = factor_three * lax.dot_general(
        low_v[...].reshape(blocks * slots, feat), up_v[...].reshape(blocks * slots, feat),
        (((0,), (0,)), ((), ())), preferred_element_type=jnp.float32,
    )
    piece = g_send.shape[1]
    for c in range(N):
        g_send[c] = grad[c * piece:(c + 1) * piece, :]

    def scatter(k, _):
        t = lax.rem(me + 1 + k, N)
        pltpu.make_async_remote_copy(
            src_ref=g_send.at[t], dst_ref=g_recv.at[me], send_sem=g_s, recv_sem=g_r,
            device_id=(lax.div(t, R), lax.rem(t, R)), device_id_type=MESH,
        ).start()
        return 0

    lax.fori_loop(0, N - 1, scatter, 0)
    g_recv[me] = g_send[me]
    whole(g_recv, N - 1, g_s, g_r).wait_recv()

    g_part[...] = jnp.sum(g_recv[...], axis=0).astype(g_part.dtype)

    def spread(k, _):
        t = lax.rem(me + 1 + k, N)
        pltpu.make_async_remote_copy(
            src_ref=g_part, dst_ref=g_all.at[me], send_sem=p_s, recv_sem=p_r,
            device_id=(lax.div(t, R), lax.rem(t, R)), device_id_type=MESH,
        ).start()
        return 0

    lax.fori_loop(0, N - 1, spread, 0)
    g_all[me] = g_part[...]

    if forward is not None:
        sends[0].wait_recv()
        forward.start()
    whole(g_all, N - 1, p_s, p_r).wait_recv()
    grad_res[...] = g_all[...].astype(jnp.float32)

    if forward is not None:
        sends[1].wait_recv()
        forward.wait_recv()
        forward.wait_send()
    else:
        for c in sends:
            c.wait_recv()
    for c in sends:
        c.wait_send()
    keep.wait()
    put.wait()
    whole(ask, D - 1, idx_s, idx_r).wait_send()
    whole(send_a, D - 1, a_s, a_r).wait_send()
    whole(send_b, D - 1, b_s, b_r).wait_send()
    whole(g_send, N - 1, g_s, g_r).wait_send()
    whole(g_all, N - 1, p_s, p_r).wait_send()


def local(D, R, h_zero, h_prev, hist_a, hist_b, tile_vals, tile_cols, pull_rows, pull_counts,
          weight_two, weight_three, grad_out):
    blocks, tiles, tile = tile_vals.shape[:3]
    feat = hist_a.shape[1]
    N = D * R
    hist_blocks = hist_a.shape[0] // tile
    piece = feat // N
    bf, f32 = jnp.bfloat16, jnp.float32
    own = (blocks, tile, feat)
    hist = (hist_blocks, tile, feat)
    slots = pull_rows.shape[2]
    pulled = (D, slots, feat)
    group = 4 if D % 4 == 0 else 1
    vm = pltpu.VMEM
    dma = pltpu.SemaphoreType.DMA
    any_spec = pl.BlockSpec(memory_space=pl.ANY)
    smem = pl.BlockSpec(memory_space=pltpu.SMEM)
    vspec = pl.BlockSpec(memory_space=pltpu.VMEM)
    out3, fresh, grad = pl.pallas_call(
        functools.partial(kernel, D, R),
        out_shape=(
            jax.ShapeDtypeStruct(own, bf),
            jax.ShapeDtypeStruct((R,) + own, bf),
            jax.ShapeDtypeStruct((N, piece, feat), f32),
        ),
        in_specs=[smem, smem, vspec] + [any_spec] * 8,
        out_specs=(any_spec, any_spec, vspec),
        scratch_shapes=[
            vm(own, bf), vm(own, bf), vm(hist, bf), vm(hist, bf), vm(tile_vals.shape, bf),
            vm((feat, feat), bf), vm((feat, feat), bf), vm(own, bf),
            vm((D, 1, slots), jnp.int32), vm((D, 1, slots), jnp.int32),
            vm((D, slots, slots), jnp.int32),
            vm(pulled, bf), vm(pulled, bf), vm(pulled, bf), vm(pulled, bf),
            vm((group * slots, feat), f32), vm(own, f32), vm(own, f32),
            vm(own, bf), vm(own, bf), vm(own, bf),
            vm((N, piece, feat), f32), vm((N, piece, feat), f32),
            vm((piece, feat), bf), vm((N, piece, feat), bf),
            dma((8,)), dma, dma, dma, dma, dma, dma,
            dma((max(R - 1, 3),)), dma((max(R - 1, 3),)), dma((2,)), dma, dma, dma, dma,
        ],
        compiler_params=pltpu.CompilerParams(
            collective_id=0, has_side_effects=True, vmem_limit_bytes=60 * 1024 * 1024
        ),
    )(
        tile_cols, pull_counts, pull_rows,
        h_zero.reshape(own), h_prev.reshape(own), hist_a.reshape(hist), hist_b.reshape(hist),
        tile_vals, weight_two, weight_three, grad_out.reshape(own),
    )
    return (
        out3.reshape(h_zero.shape),
        fresh.reshape(R * h_zero.shape[0], feat),
        grad.reshape(feat, feat),
    )


def solution(mesh):
    both = ("dev", "rep")
    return jax.shard_map(
        functools.partial(local, mesh.shape["dev"], mesh.shape["rep"]),
        mesh=mesh,
        in_specs=(
            P(both, None), P(both, None), P("dev", None), P("dev", None),
            P(both, None, None, None), P(both, None), P(both, None, None), P(both, None),
            P(), P(), P(both, None),
        ),
        out_specs=(P(both, None), P("dev", None), P()),
        check_vma=False,
    )
```

time: 247 us -> 62.8 us (0.25)
  waiting for transfers between devices: 136 us -> 0 us
  Pallas kernels: 0 us -> 56.2 us
  blocking collectives: 30.4 us -> 0 us
  local copies, waits for them, and re-layouts: 34.6 us -> 5.66 us
  other arithmetic: 17.9 us -> 0 us
  between operations: 15.7 us -> 0.64 us
  matrix products: 7.34 us -> 0 us
  starting transfers between devices: 4.23 us -> 0 us
    psum x1 -> x0, waiting for transfers between devices: 121 us -> none  [local(): grad_total = lax.psum(grad_term, ('dev', 'rep'))]
    pallas_call x0 -> x1, Pallas kernels: none -> 56.2 us  [local(): pl.pallas_call(functools.partial(kernel, D, R), out_shape=(jax.ShapeDtype...]
    all_to_all x2 -> x0, blocking collectives: 30.4 us -> none  [the longest x1 16.4 us: local(): lax.all_to_all(serve_rows(hist_a), 'dev', split_axis=0, concat_axis=0, ti...]
    gather x4 -> x0, local copies, waits for them, and re-layouts: 28.8 us -> none  [the longest x2 15.8 us: propagate(): jnp.take(blocks, columns.reshape(-1), axis=0)]
    all_to_all x1 -> x0, waiting for transfers between devices: 13.4 us -> none  [local(): lax.all_to_all(serve_rows(hist_b), 'dev', split_axis=0, concat_axis=0, ti...]
    select_n x5 -> x0, other arithmetic: 11.3 us -> none  [the longest x3 6.86 us: propagate(): jnp.take(blocks, columns.reshape(-1), axis=0)]
    dot_general x5 -> x0, matrix products: 7.34 us -> none  [the longest x2 3.85 us: propagate(): product = jnp.dot(mixed_low, weight, preferred_element_type=jnp.float32)]
    concatenate x2 -> x0, other arithmetic: 6.33 us -> none  [propagate(): jnp.concatenate([current, history, pulled.reshape(-1, feature_width)], ax...]
  transfers between devices with their start and end apart: 3 -> 0, of which waited for: 3 -> 0; matrix products, arithmetic and copies ran while one was open for 8% -> 0% of each run, Pallas kernels for 0% -> 0%
where the time goes in v1:
time: 62.8 us; the launch traced here: 62.5 us
  Pallas kernels  56.2 us (89%)
  local copies, waits for them, and re-layouts  5.66 us (9%)
  between operations  0.64 us (1%)
    pallas_call x1, Pallas kernels, local(): pl.pallas_call(functools.partial(kernel, D, R), out_shape=(jax.ShapeDtype...  56.2 us
    unnamed x5, local copies, waits for them, and re-layouts  5.66 us

profile of v1, /device:TPU:0, one launch (start us, length us, event | category | flops | bytes accessed | tf_op | source)
XLA Modules:
  0.0 62.5 jit_solution(18285650540449161360)
XLA Ops:
  0.6 56.2 %shard_map.130 = (bf16[8,128,256]{2,1,0:T(8,128)(2,1)}, bf16[4,8,128,256]{3,2,1,0:T(8,128)(2,1)}, f32[32,8,256]{2,1,0:T(8,128)}) custom-call(s32[8,12]{1,0:T(8,128)} %cols.1, s32[1,8]{1,0:T(1,128)} %counts.1, s32[1,8,128]{2,1,0:T(8,128)} %rows_in.1, bf16[8,128,256]{2,1,0:T(8,128)(2,1)} %bitcast.12, bf16[8,128,256]{2,1,0:T(8,128)(2,1)} %bitcast.13, ...), custom_call_target="tpu_custom_call" | custom-call | tf_op jit(solution)/shard_map/pallas_call | solution.py:294
  56.9 1.9 %copy.17 = bf16[1024,256]{1,0:T(8,128)(2,1)} copy(bf16[1024,256]{1,0:T(8,128)(2,1)} %bitcast.11) | data formatting | bytes 1048576
  58.7 0.0 copy-start
  58.7 3.1 %copy.18 = bf16[4096,256]{1,0:T(8,128)(2,1)} copy(bf16[4096,256]{1,0:T(8,128)(2,1)} %bitcast.8) | data formatting | bytes 4194304
  61.8 0.0 copy-done
  61.8 0.7 %copy.19 = f32[256,256]{1,0:T(8,128)} copy(f32[256,256]{1,0:T(8,128)S(1)} %bitcast.15) | data formatting | bytes 524288
Async XLA Ops:
  58.7 3.1 %copy-start = (f32[32,8,256]{2,1,0:T(8,128)S(1)}, f32[32,8,256]{2,1,0:T(8,128)}, u32[]{:S(2)}) copy-start(f32[32,8,256]{2,1,0:T(8,128)} %get-tuple-element.8) | copy-start | bytes 786436

commit v2 on v1

--- a/solution.py
+++ b/solution.py
@@ -20,8 +20,8 @@
     layer_out, hist_out, grad_res,
     zero_v, cur_v, hist_av, hist_bv, vals_v, w2_v, w3_v, up_v,
     ask, asked, col, send_a, send_b, pull_a, pull_b, acc, acc_a, acc_b,
-    fresh, low_v, out_v, g_send, g_recv, g_part, g_all,
-    local_sem, idx_s, idx_r, a_s, a_r, b_s, b_r, f_s, f_r, out_sem, g_s, g_r, p_s, p_r,
+    fresh_v, low_v, g_send, g_mate, g_recv, g_part, g_all,
+    local_sem, idx_s, idx_r, a_s, a_r, b_s, b_r, f_s, f_r, m_s, m_r, g_s, g_r, p_s, p_r,
 ):
     N = D * R
     d = lax.axis_index("dev")
@@ -62,8 +62,11 @@
     lax.fori_loop(0, D, mask_rows, 0)
     pl.semaphore_wait(barrier, N - 1)
 
+    def offset(j):
+        return D // 2 + lax.div(j + 1, 2) * (1 - 2 * lax.rem(j, 2))
+
     def send_rows(j, _):
-        p = lax.rem(d + 1 + j, D)
+        p = lax.rem(d + offset(j), D)
         pltpu.make_async_remote_copy(
             src_ref=ask.at[p], dst_ref=asked.at[d], send_sem=idx_s, recv_sem=idx_r,
             device_id=(p, r), device_id_type=MESH,
@@ -83,13 +86,13 @@
     whole(asked, D - 1, idx_s, idx_r).wait_recv()
 
     def column(j, _):
-        q = lax.rem(d + D - 1 - j + D, D)
+        q = lax.rem(d + D - offset(j), D)
         col[j] = jnp.broadcast_to(asked[q], (slots, slots)).T
         return 0
 
     lax.fori_loop(0, D, column, 0)
 
-    group = 4 if D % 4 == 0 else 1
+    group = 2 if D % 2 == 0 else 1
     chunk_blocks = 8
     depth = chunk_blocks * slots
     lanes = lax.broadcasted_iota(jnp.int32, (group * slots, depth), 1)
@@ -124,7 +127,7 @@
 
                 @pl.when(j < D - 1)
                 def _():
-                    q = lax.rem(d + D - 1 - j + D, D)
+                    q = lax.rem(d + D - offset(j), D)
                     pltpu.make_async_remote_copy(
                         src_ref=send_buf.at[j], dst_ref=pull_buf.at[d], send_sem=s, recv_sem=q_sem,
                         device_id=(q, r), device_id_type=MESH,
@@ -175,7 +178,9 @@
     factor_three = math.log(strength / 3 + 1.0)
 
     def second(i, _):
-        fresh[i] = finish(i, acc_a, pull_a, w2_v, 2, factor_two)[0]
+        rows = finish(i, acc_a, pull_a, w2_v, 2, factor_two)[0]
+        fresh_v[i] = rows
+        hist_out[r, i] = rows
         return 0
 
     lax.fori_loop(0, blocks, second, 0)
@@ -186,9 +191,10 @@
             device_id=(d, target), device_id_type=MESH,
         )
 
-    keep = pltpu.make_async_copy(fresh, hist_out.at[r], out_sem.at[0])
+    fresh = hist_out.at[r]
+    side = lax.rem(r, 2)
+    mate = r + 1 - 2 * side
     if R == 4:
-        mate = r + 1 - 2 * lax.rem(r, 2)
         across = lax.rem(r + 2, R)
         sends = [fresh_copy(fresh, r, across, 0), fresh_copy(fresh, r, mate, 1)]
         forward = fresh_copy(hist_out.at[across], across, mate, 2)
@@ -197,10 +203,9 @@
         forward = None
     for c in sends:
         c.start()
-    keep.start()
 
     def own_tile(i, _):
-        acc_b[i] += product(i, [(0, fresh[cols[i, 0]])])
+        acc_b[i] += product(i, [(0, fresh_v[cols[i, 0]])])
         return 0
 
     lax.fori_loop(0, blocks, own_tile, 0)
@@ -208,50 +213,57 @@
 
     def third(i, _):
         out, low = finish(i, acc_b, pull_b, w3_v, 3, factor_three)
-        out_v[i] = out
+        layer_out[i] = out
         low_v[i] = low
         return 0
 
     lax.fori_loop(0, blocks, third, 0)
-    put = pltpu.make_async_copy(out_v, layer_out, out_sem.at[1])
-    put.start()
 
     grad = factor_three * lax.dot_general(
         low_v[...].reshape(blocks * slots, feat), up_v[...].reshape(blocks * slots, feat),
         (((0,), (0,)), ((), ())), preferred_element_type=jnp.float32,
     )
-    piece = g_send.shape[1]
+    half = N // 2
+    piece = g_send.shape[2]
     for c in range(N):
-        g_send[c] = grad[c * piece:(c + 1) * piece, :]
+        g_send[c // half, c % half] = grad[c * piece:(c + 1) * piece, :]
+    place = d * (R // 2) + lax.div(r, 2)
+    to_mate = pltpu.make_async_remote_copy(
+        src_ref=g_send.at[1 - side], dst_ref=g_mate, send_sem=m_s, recv_sem=m_r,
+        device_id=(d, mate), device_id_type=MESH,
+    )
+    to_mate.start()
+    to_mate.wait_recv()
+    g_mate[...] += g_send[side]
 
     def scatter(k, _):
-        t = lax.rem(me + 1 + k, N)
+        t = lax.rem(place + 1 + k, half)
         pltpu.make_async_remote_copy(
-            src_ref=g_send.at[t], dst_ref=g_recv.at[me], send_sem=g_s, recv_sem=g_r,
-            device_id=(lax.div(t, R), lax.rem(t, R)), device_id_type=MESH,
+            src_ref=g_mate.at[t], dst_ref=g_recv.at[place], send_sem=g_s, recv_sem=g_r,
+            device_id=(lax.div(t, R // 2), 2 * lax.rem(t, R // 2) + side), device_id_type=MESH,
         ).start()
         return 0
 
-    lax.fori_loop(0, N - 1, scatter, 0)
-    g_recv[me] = g_send[me]
-    whole(g_recv, N - 1, g_s, g_r).wait_recv()
+    lax.fori_loop(0, half - 1, scatter, 0)
+    g_recv[place] = g_mate[place]
+    if forward is not None:
+        sends[0].wait_recv()
+        forward.start()
+    whole(g_recv, half - 1, g_s, g_r).wait_recv()
 
     g_part[...] = jnp.sum(g_recv[...], axis=0).astype(g_part.dtype)
+    mine = side * half + place
 
     def spread(k, _):
         t = lax.rem(me + 1 + k, N)
         pltpu.make_async_remote_copy(
-            src_ref=g_part, dst_ref=g_all.at[me], send_sem=p_s, recv_sem=p_r,
+            src_ref=g_part, dst_ref=g_all.at[mine], send_sem=p_s, recv_sem=p_r,
             device_id=(lax.div(t, R), lax.rem(t, R)), device_id_type=MESH,
         ).start()
         return 0
 
     lax.fori_loop(0, N - 1, spread, 0)
-    g_all[me] = g_part[...]
-
-    if forward is not None:
-        sends[0].wait_recv()
-        forward.start()
+    g_all[mine] = g_part[...]
     whole(g_all, N - 1, p_s, p_r).wait_recv()
     grad_res[...] = g_all[...].astype(jnp.float32)
 
@@ -264,13 +276,26 @@
             c.wait_recv()
     for c in sends:
         c.wait_send()
-    keep.wait()
-    put.wait()
     whole(ask, D - 1, idx_s, idx_r).wait_send()
     whole(send_a, D - 1, a_s, a_r).wait_send()
     whole(send_b, D - 1, b_s, b_r).wait_send()
-    whole(g_send, N - 1, g_s, g_r).wait_send()
+    to_mate.wait_send()
+    whole(g_recv, half - 1, g_s, g_r).wait_send()
     whole(g_all, N - 1, p_s, p_r).wait_send()
+
+
+def hand_over(parts, *refs):
+    sources, targets, sem = refs[:3], refs[3:6], refs[6]
+    outs = []
+    for n, src, dst in zip(parts, sources, targets):
+        rows = src.shape[0] // n
+        for i in range(n):
+            at = pl.ds(i * rows, rows)
+            outs.append(pltpu.make_async_copy(src.at[at], dst.at[at], sem.at[len(outs)]))
+    for c in outs:
+        c.start()
+    for c in outs:
+        c.wait()
 
 
 def local(D, R, h_zero, h_prev, hist_a, hist_b, tile_vals, tile_cols, pull_rows, pull_counts,
@@ -285,12 +310,13 @@
     hist = (hist_blocks, tile, feat)
     slots = pull_rows.shape[2]
     pulled = (D, slots, feat)
-    group = 4 if D % 4 == 0 else 1
+    group = 2 if D % 2 == 0 else 1
     vm = pltpu.VMEM
     dma = pltpu.SemaphoreType.DMA
     any_spec = pl.BlockSpec(memory_space=pl.ANY)
     smem = pl.BlockSpec(memory_space=pltpu.SMEM)
     vspec = pl.BlockSpec(memory_space=pltpu.VMEM)
+    grant = 20 * 2**20 + D * slots * (8 * feat + 4 * slots)
     out3, fresh, grad = pl.pallas_call(
         functools.partial(kernel, D, R),
         out_shape=(
@@ -299,7 +325,7 @@
             jax.ShapeDtypeStruct((N, piece, feat), f32),
         ),
         in_specs=[smem, smem, vspec] + [any_spec] * 8,
-        out_specs=(any_spec, any_spec, vspec),
+        out_specs=(vspec, vspec, vspec),
         scratch_shapes=[
             vm(own, bf), vm(own, bf), vm(hist, bf), vm(hist, bf), vm(tile_vals.shape, bf),
             vm((feat, feat), bf), vm((feat, feat), bf), vm(own, bf),
@@ -307,25 +333,40 @@
             vm((D, slots, slots), jnp.int32),
             vm(pulled, bf), vm(pulled, bf), vm(pulled, bf), vm(pulled, bf),
             vm((group * slots, feat), f32), vm(own, f32), vm(own, f32),
-            vm(own, bf), vm(own, bf), vm(own, bf),
-            vm((N, piece, feat), f32), vm((N, piece, feat), f32),
+            vm(own, bf), vm(own, bf),
+            vm((2, N // 2, piece, feat), f32), vm((N // 2, piece, feat), f32),
+            vm((N // 2, piece, feat), f32),
             vm((piece, feat), bf), vm((N, piece, feat), bf),
             dma((8,)), dma, dma, dma, dma, dma, dma,
-            dma((max(R - 1, 3),)), dma((max(R - 1, 3),)), dma((2,)), dma, dma, dma, dma,
+            dma((max(R - 1, 3),)), dma((max(R - 1, 3),)), dma, dma, dma, dma, dma, dma,
         ],
         compiler_params=pltpu.CompilerParams(
-            collective_id=0, has_side_effects=True, vmem_limit_bytes=60 * 1024 * 1024
+            collective_id=0, has_side_effects=True, vmem_limit_bytes=grant
         ),
     )(
-        tile_cols, pull_counts, pull_rows,
-        h_zero.reshape(own), h_prev.reshape(own), hist_a.reshape(hist), hist_b.reshape(hist),
-        tile_vals, weight_two, weight_three, grad_out.reshape(own),
-    )
-    return (
+        *[
+            pltpu.with_memory_space_constraint(x, pltpu.HBM)
+            for x in (
+                tile_cols, pull_counts, pull_rows, h_zero.reshape(own), h_prev.reshape(own),
+                hist_a.reshape(hist), hist_b.reshape(hist), tile_vals, weight_two, weight_three,
+                grad_out.reshape(own),
+            )
+        ]
+    )
+    flat = (
         out3.reshape(h_zero.shape),
         fresh.reshape(R * h_zero.shape[0], feat),
         grad.reshape(feat, feat),
     )
+    parts = (4, 8, 1)
+    return pl.pallas_call(
+        functools.partial(hand_over, parts),
+        out_shape=tuple(jax.ShapeDtypeStruct(x.shape, x.dtype) for x in flat),
+        in_specs=[vspec] * 3,
+        out_specs=(any_spec,) * 3,
+        scratch_shapes=[dma((sum(parts),))],
+        compiler_params=pltpu.CompilerParams(vmem_limit_bytes=8 * 1024 * 1024),
+    )(*flat)
 
 
 def solution(mesh):

time: 62.8 us -> 56.1 us (0.89)
  local copies, waits for them, and re-layouts: 5.66 us -> 0 us
  Pallas kernels: 56.2 us -> 55.2 us
    unnamed x5 -> x0, local copies, waits for them, and re-layouts: 5.66 us -> none
    pallas_call x1, Pallas kernels: 56.2 us -> 53.5 us  [local(): pl.pallas_call(functools.partial(kernel, D, R), out_shape=(jax.ShapeDtype...]
    pallas_call x0 -> x1, Pallas kernels: none -> 1.68 us  [local(): pl.pallas_call(functools.partial(hand_over, parts), out_shape=tuple((jax....]
where the time goes in v2:
time: 56.1 us; the launch traced here: 55.9 us
  Pallas kernels  55.2 us (98%)
  between operations  0.64 us (1%)
    pallas_call x1, Pallas kernels, local(): pl.pallas_call(functools.partial(kernel, D, R), out_shape=(jax.ShapeDtype...  53.5 us
    pallas_call x1, Pallas kernels, local(): pl.pallas_call(functools.partial(hand_over, parts), out_shape=tuple((jax....  1.68 us

profile of v2, /device:TPU:0, one launch (start us, length us, event | category | flops | bytes accessed | tf_op | source)
XLA Modules:
  0.0 55.9 jit_solution(7097255622310514920)
XLA Ops:
  0.6 53.5 %shard_map.130 = (bf16[8,128,256]{2,1,0:T(8,128)(2,1)S(1)}, bf16[4,8,128,256]{3,2,1,0:T(8,128)(2,1)S(1)}, f32[32,8,256]{2,1,0:T(8,128)S(1)}) custom-call(s32[8,12]{1,0:T(8,128)} %cols.1, s32[1,8]{1,0:T(1,128)} %counts.1, s32[1,8,128]{2,1,0:T(8,128)} %rows_in.1, bf16[8,128,256]{2,1,0:T(8,128)(2,1)} %bitcast.13, bf16[8,128,256]{2,1,0:T(8,128)(2,1)} %bitcast.14, ...), custom_call_target="tpu_custom_call" | custom-call | tf_op jit(solution)/shard_map/pallas_call | solution.py:320
  54.2 1.7 %shard_map.131 = (bf16[1024,256]{1,0:T(8,128)(2,1)}, bf16[4096,256]{1,0:T(8,128)(2,1)}, f32[256,256]{1,0:T(8,128)}) custom-call(bf16[1024,256]{1,0:T(8,128)(2,1)S(1)} %bitcast.9, bf16[4096,256]{1,0:T(8,128)(2,1)S(1)} %bitcast.8, f32[256,256]{1,0:T(8,128)S(1)} %bitcast.10), custom_call_target="tpu_custom_call" | custom-call | tf_op jit(solution)/shard_map/pallas_call | solution.py:362
